TPU v7x, 32 devices: a whole 2x2x4 slice. The times are simulated.
32 devices in a mesh: grp: 2 (over y), tok: 4 (over z), feat: 4 (over x, core).
Axes of the slice: x: 2, y: 2, z: 4, core: 2. Of those that a mesh axis runs over, the one named last changes fastest.
Arguments:
- acts: bfloat16 [6144, 28672], P(('grp', 'tok'), 'feat'), parts along dimension 0, may hold values from -6 to 6
- grads: bfloat16 [6144, 8192], P(('grp', 'tok'), 'feat'), parts along dimension 0, may hold values from -6 to 6
- proj_in: bfloat16 [28672, 512], P('feat'), may hold values from -0.03125 to 0.03125
- proj_out: bfloat16 [8192, 512], P('feat'), may hold values from -0.0625 to 0.0625
- doc_lengths: int32 [8], P('grp'), parts along dimension 0, may hold values from 1 to 1536, 3072 in all
- doc_owner: int32 [8], P('grp'), parts along dimension 0, may hold values from 0 to 3, as said below
Outputs:
- doc_grads: float32 [8, 512, 512], P(('grp', 'tok'), 'feat'), parts along dimension 0
There are 2 independent parts, one for each index of `grp`. A program takes and returns all parts, laid end to end along the dimension named above; an argument that names none is the same for every part. Nothing has to cross between parts.
Inputs may be any that keep to these rules, and one draw needn't show every extreme that they name: `doc_lengths`: the lengths sum to 3072; the largest is exactly 1536. `doc_owner`: every index along tok owns exactly 1 documents.
All inputs are finite; a program needn't handle non-finite values.
Results may differ from a plain program's by a relative error of at most 0.0043.
Values may be sent and summed in bfloat16 or wider, within the bound.
No kernel may reach another device: no remote copies, remote signals or barrier semaphores. Data moves between devices by JAX's collectives and lax.ppermute only.
A program may use at most 64 MiB of HBM per device.

v0:
```python
import jax
import jax.numpy as jnp
from jax import lax
from jax.sharding import PartitionSpec as P


def outer_sum(weight_cols, low_out, low_in):
    width = weight_cols.shape[1]
    row_share = low_out.shape[1]
    weighted = (low_out[:, None, :] * weight_cols[:, :, None]).reshape(
        low_out.shape[0], width * row_share
    )
    product = lax.dot_general(
        weighted, low_in, (((0,), (0,)), ((), ())), preferred_element_type=jnp.float32
    )
    return product.reshape(width, row_share, low_in.shape[1])


def shards(acts, grads, proj_in, proj_out, doc_lengths, doc_owner):
    tok_rows = acts.shape[0]
    doc_count = doc_lengths.shape[0]
    slot_count = doc_count // lax.axis_size("tok")
    part_in = jnp.dot(acts, proj_in, preferred_element_type=jnp.float32)
    part_out = jnp.dot(grads, proj_out, preferred_element_type=jnp.float32)
    full_in = lax.psum(part_in, "feat")
    grad_part = lax.psum_scatter(part_out, "feat", scatter_dimension=1, tiled=True)
    in_low = full_in.astype(jnp.bfloat16)
    out_low = grad_part.astype(jnp.bfloat16)
    doc_ends = jnp.cumsum(doc_lengths)
    doc_starts = doc_ends - doc_lengths
    doc_index = jnp.arange(doc_count, dtype=jnp.int32)
    same_owner = doc_owner[:, None] == doc_owner[None, :]
    earlier = doc_index[:, None] < doc_index[None, :]
    slot_rank = jnp.sum((same_owner & earlier).astype(jnp.int32), axis=0)
    target = doc_owner * slot_count + slot_rank
    matches = target[:, None] == doc_index[None, :]
    routing = matches.astype(jnp.bfloat16)
    own_first = lax.axis_index("tok") * slot_count
    position = lax.axis_index("tok") * tok_rows + jnp.arange(tok_rows, dtype=jnp.int32)
    member = (
        (position[:, None] >= doc_starts[None, :]) & (position[:, None] < doc_ends[None, :])
    ).astype(jnp.bfloat16)
    all_weights = jnp.dot(member, routing, preferred_element_type=jnp.float32).astype(jnp.bfloat16)
    totals = lax.psum_scatter(
        outer_sum(all_weights, out_low, in_low), "tok", scatter_dimension=0, tiled=True
    )
    slot_lengths = jnp.sum(jnp.where(matches, doc_lengths[:, None], 0), axis=0)
    own_lengths = lax.dynamic_slice_in_dim(slot_lengths, own_first, slot_count, 0)
    scaling = lax.rsqrt(own_lengths.astype(jnp.float32))
    return totals * scaling[:, None, None]


def solution(mesh):
    in_specs = (
        P(("grp", "tok"), "feat"),
        P(("grp", "tok"), "feat"),
        P("feat", None),
        P("feat", None),
        P("grp"),
        P("grp"),
    )
    out_specs = P(("grp", "tok"), "feat", None)
    return jax.shard_map(shards, mesh=mesh, in_specs=in_specs, out_specs=out_specs, check_vma=False)
```

profile of v0, /device:TPU:0, one launch (start us, length us, event | category | flops | bytes accessed | tf_op | source)
XLA Modules:
  0.0 109.7 jit_solution(2129140301364226923)
XLA Ops:
  6.5 0.0 copy-start
  6.5 0.0 copy-start.1
  6.5 0.0 reduce-scatter.3.cloned.1.call-start
  6.5 1.9 %copy-done = bf16[768,2048]{1,0:T(8,128)(2,1)S(1)} copy-done((bf16[768,2048]{1,0:T(8,128)(2,1)S(1)}, bf16[768,2048]{1,0:T(8,128)(2,1)}, u32[]{:S(2)}) %copy-start) | copy-done | bytes 3145752
  8.4 4.5 %fusion.15 = f32[768,512]{1,0:T(8,128)} fusion(bf16[768,2048]{1,0:T(8,128)(2,1)S(1)} %copy-done, bf16[2048,512]{1,0:T(8,128)(2,1)} %param.9), kind=kOutput, calls=%fused_computation.23 | convolution fusion | flops 1610612736 | bytes 6815744 | tf_op jit(solution)/shard_map/dot_general | solution.py:24
  13.0 0.0 reduce-scatter.3.cloned.1.call-update
  13.0 0.0 reduce-scatter.5.cloned.1.call-start
  13.0 0.0 copy-done.1
  13.1 0.1 convert_reduce_fusion
  13.1 0.0 copy-start.2
  13.1 11.6 %fusion.16 = f32[768,512]{1,0:T(8,128)} fusion(bf16[768,7168]{1,0:T(8,128)(2,1)} %param.6, bf16[7168,512]{1,0:T(8,128)(2,1)} %param.8), kind=kOutput, calls=%fused_computation.24 | convolution fusion | flops 5637144576 | bytes 19922944 | tf_op jit(solution)/shard_map/dot_general | solution.py:23
  24.8 0.0 copy-done.2
  24.8 0.2 reduce-window.8
  25.0 0.3 convolution_convert_fusion
  25.2 43.7 %all-reduce.1 = bf16[768,512]{1,0:T(8,128)(2,1)} all-reduce(f32[768,512]{1,0:T(8,128)} %fusion.16), channel_id=1, replica_groups=mesh['grp'=2,'tok'=4,'feat'=4] {'feat'}, use_global_device_ids=true, to_apply=%region_3.4 | all-reduce | flops 393216 | bytes 2359296 | tf_op jit(solution)/shard_map/psum | solution.py:25
  68.9 0.0 reduce-scatter.3.cloned.1.call-done
  68.9 1.0 convert_element_type.17
  70.0 0.1 copy.9
  70.1 2.7 %fusion = f32[4,128,512]{2,1,0:T(8,128)} fusion(bf16[768,512]{1,0:T(8,128)(2,1)} %all-reduce.1, bf16[768,4]{0,1:T(4,128)(2,1)S(1)} %convolution_convert_fusion, bf16[768,128]{0,1:T(8,128)(2,1)S(1)} %copy.9), kind=kOutput, calls=%fused_computation.1 | convolution fusion | flops 403046400 | bytes 2037760 | tf_op jit(solution)/shard_map/dot_general | solution.py:13
  72.8 0.0 reduce-scatter.5.cloned.1.call-update
  72.8 0.1 select_reduce_fusion
  72.9 0.6 dynamic_slice.3
  74.2 26.9 %reduce-scatter.5.cloned.1.call-done = f32[1,128,512]{2,1,0:T(8,128)} async-done(((f32[4,128,512]{2,1,0:T(8,128)}), f32[1,128,512]{2,1,0:T(8,128)}) %reduce-scatter.5.cloned.1.call-update) | async-done | bytes 262160 | tf_op jit(solution)/shard_map/reduce_scatter | solution.py:44
  101.1 1.7 %broadcast_multiply_fusion = f32[1,128,512]{2,1,0:T(8,128)} fusion(f32[1,128,512]{2,1,0:T(8,128)} %reduce-scatter.5.cloned.1.call-done, f32[]{:T(128)} %bitcast.6), kind=kLoop, calls=%fused_computation.8 | loop fusion | flops 65536 | bytes 524292 | tf_op jit(solution)/shard_map/mul | solution.py:50
  (3 shorter events, 0.0 us)
Async XLA Ops:
  6.5 1.9 %copy-start = (bf16[768,2048]{1,0:T(8,128)(2,1)S(1)}, bf16[768,2048]{1,0:T(8,128)(2,1)}, u32[]{:S(2)}) copy-start(bf16[768,2048]{1,0:T(8,128)(2,1)} %param.7) | copy-start | bytes 9437188
  6.5 6.5 %copy-start.1 = (s32[4]{0:T(128)S(1)}, s32[4]{0:T(128)}, u32[]{:S(2)}) copy-start(s32[4]{0:T(128)} %param.11) | copy-start | bytes 52
  6.5 62.4 %reduce-scatter.3.cloned.1.call-start = ((), (), s32[]{:S(2)}) async-start(), calls=%async_computation.2 | async-start | bytes 1966080 | tf_op jit(solution)/shard_map/reduce_scatter | solution.py:26
  13.0 88.2 %reduce-scatter.5.cloned.1.call-start = ((), (), s32[]{:S(2)}) async-start(), calls=%async_computation.3 | async-start | bytes 1310720 | tf_op jit(solution)/shard_map/reduce_scatter | solution.py:44
  13.1 11.6 %copy-start.2 = (s32[4]{0:T(128)S(1)}, s32[4]{0:T(128)}, u32[]{:S(2)}) copy-start(s32[4]{0:T(128)} %param.10) | copy-start | bytes 52
Sparse Core Ops, SparseCore 0:
  13.1 39.2 reduce-scatter.2
  73.0 28.1 reduce-scatter.4
where the time goes:
time: 110 us
  blocking collectives  43.7 us (40%)
  waiting for transfers between devices  27 us (25%)
  matrix products  19.1 us (17%)
  between operations  14.1 us (13%)
  other arithmetic  3.05 us (3%)
  local copies, waits for them, and re-layouts  2.62 us (2%)
    psum x1, blocking collectives, shards(): full_in = lax.psum(part_in, 'feat')  43.7 us
    reduce_scatter x1, waiting for transfers between devices, shards(): lax.psum_scatter(outer_sum(all_weights, out_low, in_low), 'tok', scatter_...  26.9 us
    dot_general x1, matrix products, shards(): part_in = jnp.dot(acts, proj_in, preferred_element_type=jnp.float32)  11.6 us
    dot_general x1, matrix products, shards(): part_out = jnp.dot(grads, proj_out, preferred_element_type=jnp.float32)  4.54 us
    dot_general x1, matrix products, outer_sum(): lax.dot_general(weighted, low_in, (((0,), (0,)), ((), ())), preferred_ele...  2.7 us
  transfers between devices with their start and end apart: 2, of which 1 were waited for; matrix products, arithmetic and copies ran while one was open for 12% of the time, Pallas kernels for 0%

commit v1 on v0

--- a/solution.py
+++ b/solution.py
@@ -22,7 +22,8 @@
     slot_count = doc_count // lax.axis_size("tok")
     part_in = jnp.dot(acts, proj_in, preferred_element_type=jnp.float32)
     part_out = jnp.dot(grads, proj_out, preferred_element_type=jnp.float32)
-    full_in = lax.psum(part_in, "feat")
+    blocks = lax.all_gather(part_in, "feat", axis=0, tiled=False)
+    full_in = blocks.sum(axis=0)
     grad_part = lax.psum_scatter(part_out, "feat", scatter_dimension=1, tiled=True)
     in_low = full_in.astype(jnp.bfloat16)
     out_low = grad_part.astype(jnp.bfloat16)

time: 110 us -> 135 us (1.23)
  waiting for transfers between devices: 27 us -> 91.5 us
  blocking collectives: 43.7 us -> 0 us
  other arithmetic: 3.05 us -> 7.72 us
    all_gather x0 -> x1, waiting for transfers between devices: none -> 46.8 us  [shards(): blocks = lax.all_gather(part_in, 'feat', axis=0, tiled=False)]
    psum x1 -> x0, blocking collectives: 43.7 us -> none  [shards(): full_in = lax.psum(part_in, 'feat')]
    reduce_scatter x1, waiting for transfers between devices: 0.01 us -> 18.6 us  [shards(): lax.psum_scatter(part_out, 'feat', scatter_dimension=1, tiled=True)]
    reduce_sum x0 -> x1, other arithmetic: none -> 4.67 us  [shards(): full_in = blocks.sum(axis=0)]
  transfers between devices with their start and end apart: 2 -> 3, of which waited for: 1 -> 3; matrix products, arithmetic and copies ran while one was open for 12% -> 10% of each run, Pallas kernels for 0% -> 0%
where the time goes in v1:
time: 135 us
  waiting for transfers between devices  91.5 us (68%)
  matrix products  19.2 us (14%)
  between operations  13.8 us (10%)
  other arithmetic  7.72 us (6%)
  local copies, waits for them, and re-layouts  2.63 us (2%)
    all_gather x1, waiting for transfers between devices, shards(): blocks = lax.all_gather(part_in, 'feat', axis=0, tiled=False)  46.8 us
    reduce_scatter x1, waiting for transfers between devices, shards(): lax.psum_scatter(outer_sum(all_weights, out_low, in_low), 'tok', scatter_...  26.1 us
    reduce_scatter x1, waiting for transfers between devices, shards(): lax.psum_scatter(part_out, 'feat', scatter_dimension=1, tiled=True)  18.6 us
    dot_general x1, matrix products, shards(): part_in = jnp.dot(acts, proj_in, preferred_element_type=jnp.float32)  11.6 us
    reduce_sum x1, other arithmetic, shards(): full_in = blocks.sum(axis=0)  4.67 us
    dot_general x1, matrix products, shards(): part_out = jnp.dot(grads, proj_out, preferred_element_type=jnp.float32)  4.61 us
  transfers between devices with their start and end apart: 3, of which 3 were waited for; matrix products, arithmetic and copies ran while one was open for 10% of the time, Pallas kernels for 0%

profile of v1, /device:TPU:0, one launch (start us, length us, event | category | flops | bytes accessed | tf_op | source)
XLA Modules:
  0.0 134.9 jit_solution(17112977618396546785)
XLA Ops:
  6.5 1.9 %copy-done = bf16[768,2048]{1,0:T(8,128)(2,1)S(1)} copy-done((bf16[768,2048]{1,0:T(8,128)(2,1)S(1)}, bf16[768,2048]{1,0:T(8,128)(2,1)}, u32[]{:S(2)}) %copy-start) | copy-done | bytes 3145752
  8.4 4.6 %fusion.15 = f32[768,512]{1,0:T(8,128)} fusion(bf16[768,2048]{1,0:T(8,128)(2,1)S(1)} %copy-done, bf16[2048,512]{1,0:T(8,128)(2,1)} %param.9), kind=kOutput, calls=%fused_computation.23 | convolution fusion | flops 1610612736 | bytes 6815744 | tf_op jit(solution)/shard_map/dot_general | solution.py:24
  13.0 0.0 reduce-scatter.3.cloned.1.call-update
  13.1 0.0 copy-start.1
  13.1 0.0 copy-start.2
  13.1 0.0 all-gather.3.cloned.1.call-start
  13.1 11.6 %fusion.16 = f32[768,512]{1,0:T(8,128)} fusion(bf16[768,7168]{1,0:T(8,128)(2,1)} %param.6, bf16[7168,512]{1,0:T(8,128)(2,1)} %param.8), kind=kOutput, calls=%fused_computation.24 | convolution fusion | flops 5637144576 | bytes 19922944 | tf_op jit(solution)/shard_map/dot_general | solution.py:23
  24.8 0.0 all-gather.3.cloned.1.call-update
  24.8 0.0 reduce-scatter.5.cloned.1.call-start
  24.9 0.1 convert_reduce_fusion
  25.0 0.0 copy-done.2
  25.0 0.2 reduce-window.8
  25.1 0.3 convolution_convert_fusion
  25.4 18.6 %reduce-scatter.3.cloned.1.call-done = f32[768,128]{1,0:T(8,128)} async-done(((f32[768,512]{1,0:T(8,128)}), f32[768,128]{1,0:T(8,128)}) %reduce-scatter.3.cloned.1.call-update) | async-done | bytes 393232 | tf_op jit(solution)/shard_map/reduce_scatter | solution.py:27
  44.0 1.0 convert_element_type.17
  45.0 0.1 copy.9
  45.1 46.8 %all-gather.3.cloned.1.call-done = f32[3072,512]{1,0:T(8,128)} async-done(((f32[768,512]{1,0:T(8,128)}), f32[3072,512]{1,0:T(8,128)}) %all-gather.3.cloned.1.call-update) | async-done | bytes 6291472 | tf_op jit(solution)/shard_map/all_gather | solution.py:25
  91.9 4.7 %reduce_sum.28 = bf16[768,512]{1,0:T(8,128)(2,1)} reduce(f32[4,768,512]{2,1,0:T(8,128)} %bitcast.19, f32[]{:T(128)} %constant.14.clone.1), dimensions={0}, to_apply=%region_3.4 | reduce | flops 1179648 | bytes 7077892 | tf_op jit(solution)/shard_map/reduce_sum | solution.py:26
  96.6 2.7 %fusion = f32[4,128,512]{2,1,0:T(8,128)} fusion(bf16[768,512]{1,0:T(8,128)(2,1)} %reduce_sum.28, bf16[768,4]{0,1:T(4,128)(2,1)S(1)} %convolution_convert_fusion, bf16[768,128]{0,1:T(8,128)(2,1)S(1)} %copy.9), kind=kOutput, calls=%fused_computation.1 | convolution fusion | flops 403046400 | bytes 2037760 | tf_op jit(solution)/shard_map/dot_general | solution.py:13
  99.3 0.0 reduce-scatter.5.cloned.1.call-update
  99.3 0.1 select_reduce_fusion
  99.4 0.6 dynamic_slice.3
  100.7 26.1 %reduce-scatter.5.cloned.1.call-done = f32[1,128,512]{2,1,0:T(8,128)} async-done(((f32[4,128,512]{2,1,0:T(8,128)}), f32[1,128,512]{2,1,0:T(8,128)}) %reduce-scatter.5.cloned.1.call-update) | async-done | bytes 262160 | tf_op jit(solution)/shard_map/reduce_scatter | solution.py:45
  126.7 1.7 %broadcast_multiply_fusion = f32[1,128,512]{2,1,0:T(8,128)} fusion(f32[1,128,512]{2,1,0:T(8,128)} %reduce-scatter.5.cloned.1.call-done, f32[]{:T(128)} %bitcast.7), kind=kLoop, calls=%fused_computation.8 | loop fusion | flops 65536 | bytes 524292 | tf_op jit(solution)/shard_map/mul | solution.py:51
  (6 shorter events, 0.0 us)
Async XLA Ops:
  6.5 1.9 %copy-start = (bf16[768,2048]{1,0:T(8,128)(2,1)S(1)}, bf16[768,2048]{1,0:T(8,128)(2,1)}, u32[]{:S(2)}) copy-start(bf16[768,2048]{1,0:T(8,128)(2,1)} %param.7) | copy-start | bytes 9437188
  6.5 37.4 %reduce-scatter.3.cloned.1.call-start = ((), (), s32[]{:S(2)}) async-start(), calls=%async_computation.2 | async-start | bytes 1966080 | tf_op jit(solution)/shard_map/reduce_scatter | solution.py:27
  13.1 11.8 %copy-start.1 = (s32[4]{0:T(128)S(1)}, s32[4]{0:T(128)}, u32[]{:S(2)}) copy-start(s32[4]{0:T(128)} %param.11) | copy-start | bytes 52
  13.1 11.9 %copy-start.2 = (s32[4]{0:T(128)S(1)}, s32[4]{0:T(128)}, u32[]{:S(2)}) copy-start(s32[4]{0:T(128)} %param.10) | copy-start | bytes 52
  13.1 78.8 %all-gather.3.cloned.1.call-start = ((), (), s32[]{:S(2)}) async-start(), calls=%async_computation.4 | async-start | bytes 7864320 | tf_op jit(solution)/shard_map/all_gather | solution.py:25
  24.8 101.9 %reduce-scatter.5.cloned.1.call-start = ((), (), s32[]{:S(2)}) async-start(), calls=%async_computation.3 | async-start | bytes 1310720 | tf_op jit(solution)/shard_map/reduce_scatter | solution.py:45
Sparse Core Ops, SparseCore 0:
  13.2 30.7 reduce-scatter.2
  45.5 46.3 all-gather.2
  99.4 27.2 reduce-scatter.4
